TPU v7x, 32 devices: a whole 2x2x4 slice. The times are simulated.
32 devices in a mesh: panel: 8 (over z, core), rhs: 4 (over y, x).
Axes of the slice: x: 2, y: 2, z: 4, core: 2. Of those that a mesh axis runs over, the one named last changes fastest.
Arguments:
- pivot_rhs: float32 [2, 2048, 512], P(None, 'panel', 'rhs'), may hold values from -6 to 6
- update_rhs: float32 [4096, 512], P('panel', 'rhs'), may hold values from -6 to 6
- parent_rhs: float32 [4096, 512], P('panel', 'rhs'), may hold values from -6 to 6
- lower_pivot: bfloat16 [2, 2048, 2048], P(None, 'panel', 'rhs'), may hold values from -1 to 1.4, as said below
- lower_update: bfloat16 [4096, 2048], P('panel', 'rhs'), may hold values from -0.125 to 0.125
- parent_lower: bfloat16 [4096, 4096], P('panel', 'rhs'), may hold values from -1 to 1.4, as said below
- parent_upper: bfloat16 [4096, 4096], P('panel', 'rhs'), may hold values from -1 to 1.4, as said below
- upper_pivot: bfloat16 [2, 2048, 2048], P(None, 'panel', 'rhs'), may hold values from -1 to 1.4, as said below
- upper_update: bfloat16 [2, 2048, 2048], P(None, 'panel', 'rhs'), may hold values from -0.125 to 0.125
- maps: int32 [4096], replicated, may hold values from 0 to 4095, as said below
Outputs:
- parent_solution: float32 [4096, 512], P('panel', 'rhs')
- child_solution: float32 [2, 2048, 512], P(None, 'panel', 'rhs')
Inputs may be any that keep to these rules, and one draw needn't show every extreme that they name: `maps`: for each child k, entry k * 2048 + i is 2 * i + b with b equal to 0 or 1; both values of b occur for each child in every draw. `lower_pivot`: each block is lower triangular, diagonal 0.6 to 1.4. `upper_pivot`: each block is upper triangular, diagonal 0.6 to 1.4. `parent_lower`: lower triangular, diagonal 0.6 to 1.4. `parent_upper`: upper triangular, diagonal 0.6 to 1.4.
All inputs are finite; a program needn't handle non-finite values.
Results may differ from a plain program's by a relative error of at most 0.0054.
Values may be sent and summed in bfloat16 or wider, within the bound.
A program may use at most 64 MiB of HBM per device.

v0:
```python
import functools

import jax
import jax.numpy as jnp
from jax import lax
from jax.experimental import pallas as pl
from jax.experimental.pallas import tpu as pltpu
from jax.sharding import PartitionSpec as P

BF = jnp.bfloat16
F32 = jnp.float32
MESH = pl.DeviceIdType.MESH


def dot(left, right):
    return jnp.dot(left, right, preferred_element_type=F32)


def kernel(
    panels,
    cols,
    pivot_rhs,
    update_rhs,
    parent_rhs,
    lower_pivot,
    lower_update,
    parent_lower,
    parent_upper,
    upper_pivot,
    upper_update,
    row_map,
    col_map,
    parent_out,
    child_out,
    pin,
    phalf,
    vec,
    x_pin,
    x_half,
    x_par,
    s_up,
    r_up,
    s_piv,
    r_piv,
    s_par,
    r_par,
    s_ch,
    r_ch,
    uhalf,
    moved,
    picked,
    direct,
    par_sum,
    spread_sum,
    child_sum,
    g_send,
    g_recv,
    f_send,
    rs_send,
    rs_recv,
    sh_send,
    sh_recv,
):
    me_p, me_r = lax.axis_index("panel"), lax.axis_index("rhs")
    total = panels * cols
    me = me_p * cols + me_r
    core = lax.rem(me_p, 2)
    mate = me_p + 1 - 2 * core
    per = panels // cols
    half = panels // 2
    m = parent_rhs.shape[0]
    mk = pivot_rhs.shape[1]
    child = me_p // half

    barrier = pltpu.get_barrier_semaphore()

    @pl.loop(1, total)
    def _(step):
        other = lax.rem(me + step, total)
        pl.semaphore_signal(
            barrier,
            inc=1,
            device_id=(other // cols, lax.rem(other, cols)),
            device_id_type=MESH,
        )

    pin[...] = pivot_rhs[...].astype(BF)
    direct[...] = jnp.zeros_like(direct)
    pl.semaphore_wait(barrier, total - 1)

    group = me_p // per
    last = cols - 1

    def every(source, goal):
        return None

    def below(source, goal):
        return goal >= source

    def above(source, goal):
        return goal <= source

    def guard(condition, action):
        if condition is None:
            action()
        else:
            pl.when(condition)(action)

    def both(first, second):
        return second if first is None else jnp.logical_and(first, second)

    def spot(buffer, depth, column, part, lead):
        rows = pl.ds(pl.multiple_of(part * depth, depth), depth)
        return buffer.at[column, slice(None) if lead is None else pl.ds(lead, 1), rows, :]

    class Gather:
        def __init__(self, stage, block, buffer, depth, keep, lead):
            self.stage, self.block, self.buffer, self.depth = stage, block, buffer, depth
            self.keep, self.lead = keep, lead
            self.active = keep(me_r, group)

        def place(self, column, part, panel):
            return spot(self.buffer, self.depth, column, part, self.lead(panel))

        def piece(self, panel):
            lead = self.lead(panel)
            return self.block if lead is None else self.block.at[pl.ds(lead, 1)]

        def goal(self, step):
            return lax.rem(me_p // 2 + step, half) * 2 + core

        def copy(self, step):
            goal = self.goal(step)
            return pltpu.make_async_remote_copy(
                src_ref=self.piece(goal),
                dst_ref=self.place(me_r, lax.rem(me_p, per), goal),
                send_sem=g_send.at[self.stage, step],
                recv_sem=g_recv.at[self.stage, me_r, lax.rem(me_p, per)],
                device_id=(goal, group),
                device_id_type=MESH,
            )

        def sends(self, action):
            for step in list(range(1, half)) + [0]:
                condition = self.keep(group, self.goal(step) // per)
                if step == 0:
                    condition = both(condition, group != me_r)
                guard(condition, functools.partial(action, step))

        def start(self):
            self.sends(lambda step: self.copy(step).start())

            @pl.when(group == me_r)
            def _():
                part = lax.rem(me_p, per)
                pltpu.make_async_copy(
                    self.piece(me_p),
                    self.place(me_r, part, me_p),
                    g_recv.at[self.stage, me_r, part],
                ).start()

        def landed(self, column, part):
            place = self.place(column, part, me_p)
            pltpu.make_async_copy(place, place, g_recv.at[self.stage, column, part]).wait()

        def forward(self, step, pair):
            column = lax.rem(me_r + 1 + step, cols)
            part = 2 * pair + core
            return pltpu.make_async_remote_copy(
                src_ref=self.place(column, part, me_p),
                dst_ref=self.place(column, part, me_p),
                send_sem=f_send.at[self.stage, step, pair],
                recv_sem=g_recv.at[self.stage, column, part],
                device_id=(mate, me_r),
                device_id_type=MESH,
            )

        def pass_on(self):
            def action():
                for step in [last] + list(range(last)):
                    for pair in range(per // 2):
                        self.landed(lax.rem(me_r + 1 + step, cols), 2 * pair + core)
                        self.forward(step, pair).start()

            guard(self.active, action)

        def arrive(self, step):
            column = lax.rem(me_r + 1 + step, cols)
            for pair in range(per // 2):
                self.landed(column, 2 * pair + 1 - core)
            return column

        def finish(self):
            self.sends(lambda step: self.copy(step).wait_send())

            def action():
                for step in range(cols):
                    for pair in range(per // 2):
                        self.forward(step, pair).wait_send()

            guard(self.active, action)

    class Scatter:
        def __init__(self, stage, source, target, keep):
            self.stage, self.source, self.target, self.keep = stage, source, target, keep
            self.active = keep(me_r, group)

        def copy(self, step):
            return pltpu.make_async_remote_copy(
                src_ref=self.source.at[step],
                dst_ref=self.target.at[step],
                send_sem=rs_send.at[self.stage, step],
                recv_sem=rs_recv.at[self.stage, step],
                device_id=(me_p, lax.rem(me_r + 1 + step, cols)),
                device_id_type=MESH,
            )

        def add(self, total_ref):
            for step in range(last):
                sender = lax.rem(me_r + last - step, cols)

                def action(step=step):
                    self.copy(step).wait_recv()
                    total_ref[...] += self.target[step].astype(F32)

                guard(self.keep(sender, group), action)

        def finish(self):
            def action():
                for step in range(last):
                    self.copy(step).wait_send()

            guard(self.active, action)

    def targets(ref, k, index, size, base):
        if ref.shape[0] == 2:
            return ref[k : k + 1, :]
        start = pl.multiple_of(k * (ref.shape[1] // 2) + index * size, 128)
        return ref[:, pl.ds(start, size)] - base

    def whole(panel):
        return None

    def same(panel):
        return panel // half

    def other(panel):
        return 1 - panel // half

    g_own = Gather(0, pin, x_pin, mk, every, same)
    g_other = Gather(5, pin, x_pin, mk, below, other)
    g_low = Gather(1, vec.at[0], x_par.at[0], m, below, whole)
    g_half = Gather(2, phalf, x_half, mk, above, whole)
    g_up = Gather(3, vec.at[1], x_par.at[1], m, above, whole)
    g_all = Gather(4, vec.at[2], x_par.at[2], m, every, whole)
    t_up = Scatter(0, s_up, r_up, every)
    t_piv = Scatter(1, s_piv, r_piv, below)
    t_low = Scatter(2, s_par.at[0], r_par.at[0], below)
    t_high = Scatter(3, s_par.at[1], r_par.at[1], above)
    t_child = Scatter(4, s_ch, r_ch, every)

    g_own.start()
    g_other.start()

    width = upper_update.shape[2]
    for k in range(2):
        rows = lax.broadcasted_iota(jnp.int32, (per * m, width), 0)
        chosen = (rows == targets(col_map, k, me_r, width, me_r * per * m)).astype(F32).astype(BF)
        picked[k] = lax.dot_general(
            upper_update[k], chosen, (((1,), (1,)), ((), ())), preferred_element_type=F32
        ).astype(BF)
    spread_sum[...] = parent_rhs[...]

    g_own.pass_on()
    for step in range(cols):
        column = g_own.arrive(step)
        value = dot(lower_update[...], x_pin[column, child])
        if step < last:
            s_up[step] = value.astype(BF)
            t_up.copy(step).start()
        else:
            par_sum[...] = update_rhs[...] + value
    g_other.pass_on()
    t_up.add(par_sum)
    update = par_sum[...].astype(BF)
    uhalf[0] = update[: m // 2]
    uhalf[1] = update[m // 2 :]
    first = lax.rem(me_p, half) * 2

    def shuffle(side):
        return pltpu.make_async_remote_copy(
            src_ref=uhalf.at[side],
            dst_ref=moved.at[child],
            send_sem=sh_send.at[side],
            recv_sem=sh_recv.at[child],
            device_id=(first + side, me_r),
            device_id_type=MESH,
        )

    for side in range(2):

        @pl.when(first + side != me_p)
        def _():
            shuffle(side).start()

        @pl.when(first + side == me_p)
        def _():
            pltpu.make_async_copy(uhalf.at[side], moved.at[child], sh_recv.at[child]).start()

    child_sum[...] = jnp.zeros_like(child_sum)

    def pivots():
        for step in range(cols):
            column = g_other.arrive(step)
            for k in range(2):
                value = dot(lower_pivot[k], x_pin[column, k])
                if step < last:
                    s_piv[step, k] = value.astype(BF)
                else:
                    child_sum[k] = value
            if step < last:
                t_piv.copy(step).start()

    guard(g_other.active, pivots)

    rows = lax.broadcasted_iota(jnp.int32, (m, m // 2), 0)
    for k in range(2):
        pltpu.make_async_copy(moved.at[k], moved.at[k], sh_recv.at[k]).wait()
        chosen = (rows == targets(row_map, k, me_p, m // 2, me_p * m)).astype(F32).astype(BF)
        spread_sum[...] += dot(chosen, moved[k])
    vec[0, 0] = spread_sum[...].astype(BF)
    g_low.start()

    t_piv.add(child_sum)
    phalf[...] = child_sum[...].astype(BF)
    g_half.start()

    def parent(level, gather, scatter, factor):
        par_sum[...] = jnp.zeros_like(par_sum)
        gather.pass_on()

        def action():
            for step in range(cols):
                column = gather.arrive(step)
                value = dot(factor[...], x_par[level, column, 0])
                if step < last:
                    s_par[level, step] = value.astype(BF)
                    scatter.copy(step).start()
                else:
                    par_sum[...] = value

        guard(gather.active, action)
        scatter.add(par_sum)
        vec[level + 1, 0] = par_sum[...].astype(BF)

    parent(0, g_low, t_low, parent_lower)
    g_up.start()
    g_half.pass_on()

    def known():
        for step in range(cols):
            column = g_half.arrive(step)
            for k in range(2):
                direct[step, k] = dot(upper_pivot[k], x_half[column, k])

    guard(g_half.active, known)
    parent(1, g_up, t_high, parent_upper)
    g_all.start()
    parent_out[...] = par_sum[...]

    g_all.pass_on()
    for step in range(cols):
        column = g_all.arrive(step)
        for k in range(2):
            value = direct[step, k] + dot(picked[k], x_par[2, column, 0])
            if step < last:
                s_ch[step, k] = value.astype(BF)
            else:
                child_out[k] = value
        if step < last:
            t_child.copy(step).start()
    for gather in (g_own, g_other, g_low, g_half, g_up, g_all):
        gather.finish()
    for side in range(2):

        @pl.when(first + side != me_p)
        def _():
            shuffle(side).wait_send()

    t_child.add(child_out)
    for scatter in (t_up, t_piv, t_low, t_high, t_child):
        scatter.finish()


def shards(panels, cols, *arguments):
    *arrays, maps = arguments
    m, width = arrays[1].shape
    mk = arrays[0].shape[1]
    per = panels // cols
    sides = maps.reshape(2, -1)
    me_p, me_r = lax.axis_index("panel"), lax.axis_index("rhs")
    wide = arrays[8].shape[2]

    def cut(index, size, base):
        if size % 128 == 0:
            return maps.reshape(1, -1)
        return lax.dynamic_slice_in_dim(sides, index * size, size, 1) - base

    row_map = cut(me_p, m // 2, me_p * m)
    col_map = cut(me_r, wide, me_r * per * m)
    vm = pltpu.VMEM
    dma = pltpu.SemaphoreType.DMA
    return pl.pallas_call(
        functools.partial(kernel, panels, cols),
        out_shape=(
            jax.ShapeDtypeStruct((m, width), F32),
            jax.ShapeDtypeStruct((2, mk, width), F32),
        ),
        in_specs=[pl.BlockSpec(memory_space=pltpu.VMEM)] * 11,
        out_specs=(pl.BlockSpec(memory_space=pltpu.VMEM),) * 2,
        scratch_shapes=[
            vm((2, mk, width), BF),
            vm((2, mk, width), BF),
            vm((3, 1, m, width), BF),
            vm((cols, 2, per * mk, width), BF),
            vm((cols, 2, per * mk, width), BF),
            vm((3, cols, 1, per * m, width), BF),
            vm((cols - 1, m, width), BF),
            vm((cols - 1, m, width), BF),
            vm((cols - 1, 2, mk, width), BF),
            vm((cols - 1, 2, mk, width), BF),
            vm((2, cols - 1, m, width), BF),
            vm((2, cols - 1, m, width), BF),
            vm((cols - 1, 2, mk, width), BF),
            vm((cols - 1, 2, mk, width), BF),
            vm((2, m // 2, width), BF),
            vm((2, m // 2, width), BF),
            vm((2, mk, per * m), BF),
            vm((cols, 2, mk, width), F32),
            vm((m, width), F32),
            vm((m, width), F32),
            vm((2, mk, width), F32),
            dma((6, panels // 2)),
            dma((6, cols, per)),
            dma((6, cols, per // 2)),
            dma((5, cols - 1)),
            dma((5, cols - 1)),
            dma((2,)),
            dma((2,)),
        ],
        compiler_params=pltpu.CompilerParams(
            collective_id=0, has_side_effects=True, vmem_limit_bytes=60 * 1024 * 1024
        ),
    )(*arrays, row_map, col_map)


def solution(mesh):
    panels, cols = mesh.shape["panel"], mesh.shape["rhs"]
    placed = (
        P(None, "panel", "rhs"),
        P("panel", "rhs"),
        P("panel", "rhs"),
        P(None, "panel", "rhs"),
        P("panel", "rhs"),
        P("panel", "rhs"),
        P("panel", "rhs"),
        P(None, "panel", "rhs"),
        P(None, "panel", "rhs"),
        P(),
    )
    return jax.shard_map(
        functools.partial(shards, panels, cols),
        mesh=mesh,
        in_specs=placed,
        out_specs=(P("panel", "rhs"), P(None, "panel", "rhs")),
        check_vma=False,
    )
```

profile of v0, /device:TPU:24, one launch (start us, length us, event | category | flops | bytes accessed | tf_op | source)
XLA Modules:
  0.0 107.9 jit_solution(1938642734498128057)
XLA Ops:
  0.6 104.8 %shard_map.113 = (f32[512,128]{1,0:T(8,128)}, f32[2,256,128]{2,1,0:T(8,128)}) custom-call(f32[2,256,128]{2,1,0:T(8,128)} %pivot_rhs.1, f32[512,128]{1,0:T(8,128)} %update_rhs.1, f32[512,128]{1,0:T(8,128)} %parent_rhs.1, bf16[2,256,512]{2,1,0:T(8,128)(2,1)} %lower_pivot.1, bf16[512,512]{1,0:T(8,128)(2,1)} %lower_update.1, bf16[512,1024]{1,0:T(8,128)(2,1)} %parent_lower.1, ...), custom_call_target="tpu_custom_call" | custom-call | tf_op jit(solution)/shard_map/pallas_call | solution.py:413
  105.4 0.0 copy-start
  105.5 1.7 %copy.14 = f32[512,128]{1,0:T(8,128)} copy(f32[512,128]{1,0:T(8,128)} %get-tuple-element.4) | data formatting | bytes 524288
  107.2 0.0 copy-done
  107.2 0.7 copy.15
Async XLA Ops:
  105.4 1.7 %copy-start = (f32[2,256,128]{2,1,0:T(8,128)S(1)}, f32[2,256,128]{2,1,0:T(8,128)}, u32[]{:S(2)}) copy-start(f32[2,256,128]{2,1,0:T(8,128)} %get-tuple-element.5) | copy-start | bytes 786436
where the time goes:
time: 108 us
  Pallas kernels  105 us (97%)
  local copies, waits for them, and re-layouts  2.42 us (2%)
    pallas_call x1, Pallas kernels, shards(): pl.pallas_call(functools.partial(kernel, panels, cols), out_shape=(jax.Sh...  105 us
    unnamed x4, local copies, waits for them, and re-layouts  2.42 us

commit v1 on v0

--- a/solution.py
+++ b/solution.py
@@ -16,7 +16,7 @@
     return jnp.dot(left, right, preferred_element_type=F32)
 
 
-def kernel(
+def plain_kernel(
     panels,
     cols,
     pivot_rhs,
@@ -392,7 +392,7 @@
         scatter.finish()
 
 
-def shards(panels, cols, *arguments):
+def plain_shards(panels, cols, *arguments):
     *arrays, maps = arguments
     m, width = arrays[1].shape
     mk = arrays[0].shape[1]
@@ -411,7 +411,7 @@
     vm = pltpu.VMEM
     dma = pltpu.SemaphoreType.DMA
     return pl.pallas_call(
-        functools.partial(kernel, panels, cols),
+        functools.partial(plain_kernel, panels, cols),
         out_shape=(
             jax.ShapeDtypeStruct((m, width), F32),
             jax.ShapeDtypeStruct((2, mk, width), F32),
@@ -454,6 +454,527 @@
     )(*arrays, row_map, col_map)
 
 
+SPLIT = 2
+
+
+def dot_rows(left, right):
+    return lax.dot_general(left, right, (((1,), (1,)), ((), ())), preferred_element_type=F32)
+
+
+def split_kernel(
+    panels,
+    cols,
+    pivot_rhs,
+    update_rhs,
+    parent_rhs,
+    lower_pivot,
+    lower_update,
+    parent_lower,
+    parent_upper,
+    upper_pivot,
+    upper_update,
+    row_map,
+    col_map,
+    parent_out,
+    child_out,
+    pin,
+    x_pin,
+    uhalf,
+    moved,
+    chosen,
+    vec,
+    x_par,
+    phalf,
+    x_half,
+    picked,
+    direct,
+    s_up,
+    r_up,
+    s_piv,
+    r_piv,
+    s_par,
+    r_par,
+    s_ch,
+    r_ch,
+    own_up,
+    own_piv,
+    own_par,
+    own_ch,
+    rhs_up,
+    rhs_par,
+    g_send,
+    g_recv,
+    f_send,
+    rs_send,
+    rs_recv,
+    sh_send,
+    sh_recv,
+):
+    me_p, me_r = lax.axis_index("panel"), lax.axis_index("rhs")
+    total = panels * cols
+    me = me_p * cols + me_r
+    core = lax.rem(me_p, 2)
+    mate = me_p + 1 - 2 * core
+    half = panels // 2
+    m, width = parent_rhs.shape
+    mk = pivot_rhs.shape[1]
+    wq = width // SPLIT
+    child = me_p // half
+    group = me_p // 2
+    last = cols - 1
+    chunks = range(SPLIT)
+
+    barrier = pltpu.get_barrier_semaphore()
+
+    @pl.loop(1, total)
+    def _(step):
+        other = lax.rem(me + step, total)
+        pl.semaphore_signal(
+            barrier,
+            inc=1,
+            device_id=(other // cols, lax.rem(other, cols)),
+            device_id_type=MESH,
+        )
+
+    for k in range(2):
+        turned = pivot_rhs[k].T.astype(BF)
+        for q in chunks:
+            pin[k, q] = turned[q * wq : (q + 1) * wq]
+    with jax.named_scope("barrier"):
+        pl.semaphore_wait(barrier, total - 1)
+
+    def every(source, goal):
+        return None
+
+    def below(source, goal):
+        return goal >= source
+
+    def above(source, goal):
+        return goal <= source
+
+    def guard(condition, action):
+        if condition is None:
+            action()
+        else:
+            pl.when(condition)(action)
+
+    def both(first, second):
+        return second if first is None else jnp.logical_and(first, second)
+
+    sent_place = lax.rem(me_r - group - 1 + 2 * cols, cols)
+
+    class Gather:
+        def __init__(self, stage, piece, place, keep):
+            self.stage, self.piece, self.place, self.keep = stage, piece, place, keep
+            self.active = keep(me_r, group)
+
+        def goal(self, step):
+            return lax.rem(group + step, half) * 2 + core
+
+        def copy(self, q, step):
+            goal = self.goal(step)
+            return pltpu.make_async_remote_copy(
+                src_ref=self.piece(q, goal),
+                dst_ref=self.place(q, core, sent_place, goal),
+                send_sem=g_send.at[self.stage, q, step],
+                recv_sem=g_recv.at[self.stage, q, sent_place, core],
+                device_id=(goal, group),
+                device_id_type=MESH,
+            )
+
+        def sends(self, action):
+            for step in list(range(1, half)) + [0]:
+                condition = self.keep(group, self.goal(step) // 2)
+                if step == 0:
+                    condition = both(condition, group != me_r)
+                guard(condition, functools.partial(action, step))
+
+        def start(self, q):
+            self.sends(lambda step: self.copy(q, step).start())
+
+            @pl.when(group == me_r)
+            def _():
+                pltpu.make_async_copy(
+                    self.piece(q, me_p),
+                    self.place(q, core, last, me_p),
+                    g_recv.at[self.stage, q, last, core],
+                ).start()
+
+        def landed(self, q, spot, part):
+            place = self.place(q, part, spot, me_p)
+            pltpu.make_async_copy(place, place, g_recv.at[self.stage, q, spot, part]).wait()
+
+        def forward(self, q, spot):
+            return pltpu.make_async_remote_copy(
+                src_ref=self.place(q, core, spot, me_p),
+                dst_ref=self.place(q, core, spot, me_p),
+                send_sem=f_send.at[self.stage, q, spot],
+                recv_sem=g_recv.at[self.stage, q, spot, core],
+                device_id=(mate, me_r),
+                device_id_type=MESH,
+            )
+
+        def pass_on(self, q):
+            def action():
+                for spot in [last] + list(range(last)):
+                    self.landed(q, spot, core)
+                    self.forward(q, spot).start()
+
+            guard(self.active, action)
+
+        def arrive(self, q):
+            for spot in range(cols):
+                self.landed(q, spot, 1 - core)
+
+        def finish(self, q):
+            self.sends(lambda step: self.copy(q, step).wait_send())
+
+            def action():
+                for spot in range(cols):
+                    self.forward(q, spot).wait_send()
+
+            guard(self.active, action)
+
+    class Scatter:
+        def __init__(self, stage, source, target, keep):
+            self.stage, self.source, self.target, self.keep = stage, source, target, keep
+            self.active = keep(me_r, group)
+
+        def copy(self, q, step):
+            return pltpu.make_async_remote_copy(
+                src_ref=self.source(q).at[step],
+                dst_ref=self.target(q).at[step],
+                send_sem=rs_send.at[self.stage, q, step],
+                recv_sem=rs_recv.at[self.stage, q, step],
+                device_id=(me_p, lax.rem(me_r + 1 + step, cols)),
+                device_id_type=MESH,
+            )
+
+        def give(self, q, value, own):
+            rows = value.shape[0] // cols
+            for step in range(last):
+                self.source(q)[step] = value[step * rows : (step + 1) * rows].astype(BF)
+                self.copy(q, step).start()
+            own[...] = value[last * rows :]
+
+        def add(self, q, total_ref):
+            for step in range(last):
+                sender = lax.rem(me_r + last - step, cols)
+
+                def action(step=step):
+                    self.copy(q, step).wait_recv()
+                    total_ref[...] += self.target(q)[step].astype(F32)
+
+                guard(self.keep(sender, group), action)
+
+        def finish(self, q):
+            def action():
+                for step in range(last):
+                    self.copy(q, step).wait_send()
+
+            guard(self.active, action)
+
+    def targets(ref, k, index, size, base):
+        if ref.shape[0] == 2:
+            return ref[k : k + 1, :]
+        start = pl.multiple_of(k * (ref.shape[1] // 2) + index * size, 128)
+        return ref[:, pl.ds(start, size)] - base
+
+    def same(panel):
+        return panel // half
+
+    def other(panel):
+        return 1 - panel // half
+
+    def pins(side):
+        return (
+            lambda q, goal: pin.at[side(goal), q],
+            lambda q, part, spot, goal: x_pin.at[side(goal), q, part, spot],
+        )
+
+    def level_parts(level):
+        return (
+            lambda q, goal: vec.at[level, q],
+            lambda q, part, spot, goal: x_par.at[level, q, part, spot],
+        )
+
+    g_own = Gather(0, *pins(same), every)
+    g_other = Gather(5, *pins(other), below)
+    g_low = Gather(1, *level_parts(0), below)
+    g_up = Gather(3, *level_parts(1), above)
+    g_all = Gather(4, *level_parts(2), every)
+    g_half = Gather(
+        2, lambda q, goal: phalf, lambda q, part, spot, goal: x_half.at[part, spot], above
+    )
+    t_up = Scatter(0, lambda q: s_up.at[q], lambda q: r_up.at[q], every)
+    t_piv = Scatter(1, lambda q: s_piv, lambda q: r_piv, below)
+    t_low = Scatter(2, lambda q: s_par.at[0, q], lambda q: r_par.at[0, q], below)
+    t_high = Scatter(3, lambda q: s_par.at[1, q], lambda q: r_par.at[1, q], above)
+    t_child = Scatter(4, lambda q: s_ch.at[q], lambda q: r_ch.at[q], every)
+
+    def gathered(block):
+        return block.reshape(cols * block.shape[1], block.shape[2])
+
+    for q in chunks:
+        g_own.start(q)
+
+    rhs_up[...] = update_rhs[...].T
+    rhs_par[...] = parent_rhs[...].T
+    own_par[...] = jnp.zeros_like(own_par)
+    own_piv[...] = jnp.zeros_like(own_piv)
+    direct[...] = jnp.zeros_like(direct)
+    rows = lax.broadcasted_iota(jnp.int32, (m, m // 2), 0)
+    for k in range(2):
+        chosen[k] = (rows == targets(row_map, k, me_p, m // 2, me_p * m)).astype(F32).astype(BF)
+
+    for q in chunks:
+        with jax.named_scope("s1_pass"):
+            g_own.pass_on(q)
+    for q in chunks:
+        with jax.named_scope("s1_arrive"):
+            g_own.arrive(q)
+        with jax.named_scope("s1_comp"):
+            value = sum(
+                dot_rows(gathered(x_pin[child, q, part]), lower_update[:, part * mk : (part + 1) * mk])
+                for part in range(2)
+            )
+            t_up.give(q, value, own_up.at[q])
+    for q in chunks:
+        g_other.start(q)
+
+    wide = upper_update.shape[2]
+    with jax.named_scope("picked"):
+        for k in range(2):
+            rows = lax.broadcasted_iota(jnp.int32, (2 * m, wide), 0)
+            hot = (rows == targets(col_map, k, me_r, wide, me_r * 2 * m)).astype(F32).astype(BF)
+            picked[k] = dot_rows(upper_update[k], hot).astype(BF)
+
+    first = lax.rem(me_p, half) * 2
+
+    def shuffle(q, side):
+        return pltpu.make_async_remote_copy(
+            src_ref=uhalf.at[q, side],
+            dst_ref=moved.at[q, child],
+            send_sem=sh_send.at[q, side],
+            recv_sem=sh_recv.at[q, child],
+            device_id=(first + side, me_r),
+            device_id_type=MESH,
+        )
+
+    for q in chunks:
+        own_up[q] += rhs_up[q * wq : (q + 1) * wq]
+        with jax.named_scope("s1_add"):
+            t_up.add(q, own_up.at[q])
+        update = own_up[q].astype(BF)
+        for side in range(2):
+            uhalf[q, side] = update[:, side * (m // 2) : (side + 1) * (m // 2)]
+
+            @pl.when(first + side != me_p)
+            def _():
+                shuffle(q, side).start()
+
+            @pl.when(first + side == me_p)
+            def _():
+                pltpu.make_async_copy(uhalf.at[q, side], moved.at[q, child], sh_recv.at[q, child]).start()
+
+    for q in chunks:
+        value = rhs_par[q * wq : (q + 1) * wq]
+        for k in range(2):
+            with jax.named_scope("moved"):
+                pltpu.make_async_copy(moved.at[q, k], moved.at[q, k], sh_recv.at[q, k]).wait()
+            value = value + dot_rows(moved[q, k], chosen[k])
+        vec[0, q] = value.astype(BF)
+        g_low.start(q)
+
+    for q in chunks:
+        with jax.named_scope("other_pass"):
+            g_other.pass_on(q)
+
+    def pivots():
+        for q in chunks:
+            g_other.arrive(q)
+        parts = []
+        for k in range(2):
+            sums = []
+            for q in chunks:
+                sums.append(
+                    sum(
+                        dot_rows(gathered(x_pin[k, q, part]), lower_pivot[k, :, part * mk : (part + 1) * mk])
+                        for part in range(2)
+                    ).reshape(cols, wq, mk)
+                )
+            parts.append(sums)
+        for step in range(cols):
+            for k in range(2):
+                for q in chunks:
+                    place = (slice(q * wq, (q + 1) * wq), slice(k * mk, (k + 1) * mk))
+                    if step < last:
+                        s_piv[(step,) + place] = parts[k][q][step].astype(BF)
+                    else:
+                        own_piv[place] = parts[k][q][step]
+            if step < last:
+                t_piv.copy(0, step).start()
+
+    with jax.named_scope("pivots"):
+        guard(g_other.active, pivots)
+
+    def multiply(level, gather, scatter, factor, q):
+        def action():
+            with jax.named_scope("arrive"):
+                gather.arrive(q)
+            value = sum(
+                dot_rows(gathered(x_par[level, q, part]), factor[:, part * m : (part + 1) * m])
+                for part in range(2)
+            )
+            scatter.give(q, value, own_par.at[level, q])
+
+        guard(gather.active, action)
+
+    def combine(level, scatter, following, q):
+        scatter.add(q, own_par.at[level, q])
+        vec[level + 1, q] = own_par[level, q].astype(BF)
+        following.start(q)
+
+    def parent(level, gather, scatter, factor, following, name):
+        for q in chunks:
+            with jax.named_scope(name + "_pass"):
+                gather.pass_on(q)
+            if q:
+                with jax.named_scope(name + "_add"):
+                    combine(level, scatter, following, q - 1)
+            with jax.named_scope(name + "_mul"):
+                multiply(level, gather, scatter, factor, q)
+        with jax.named_scope(name + "_add"):
+            combine(level, scatter, following, SPLIT - 1)
+
+    parent(0, g_low, t_low, parent_lower, g_up, "low")
+
+    with jax.named_scope("piv_add"):
+        t_piv.add(0, own_piv)
+    phalf[...] = own_piv[...].astype(BF)
+    g_half.start(0)
+
+    parent(1, g_up, t_high, parent_upper, g_all, "up")
+
+    with jax.named_scope("half_pass"):
+        g_half.pass_on(0)
+
+    def known():
+        g_half.arrive(0)
+        for k in range(2):
+            value = sum(
+                dot_rows(
+                    gathered(x_half[part, :, :, k * mk : (k + 1) * mk]),
+                    upper_pivot[k, :, part * mk : (part + 1) * mk],
+                )
+                for part in range(2)
+            )
+            direct[:, :, k * mk : (k + 1) * mk] = value.reshape(cols, width, mk)
+
+    with jax.named_scope("known"):
+        guard(g_half.active, known)
+    parent_out[...] = own_par[1].reshape(width, m).T
+
+    for q in chunks:
+        with jax.named_scope("all_pass"):
+            g_all.pass_on(q)
+        with jax.named_scope("all_arrive"):
+            g_all.arrive(q)
+        with jax.named_scope("all_comp"):
+            for k in range(2):
+                lanes = slice(k * mk, (k + 1) * mk)
+                value = gathered(direct[:, q * wq : (q + 1) * wq, lanes]) + sum(
+                    dot_rows(gathered(x_par[2, q, part]), picked[k, :, part * m : (part + 1) * m])
+                    for part in range(2)
+                )
+                for step in range(last):
+                    s_ch[q, step, :, lanes] = value[step * wq : (step + 1) * wq].astype(BF)
+                own_ch[q, :, lanes] = value[last * wq :]
+            for step in range(last):
+                t_child.copy(q, step).start()
+
+    with jax.named_scope("gfinish"):
+        for q in chunks:
+            for gather in (g_own, g_other, g_low, g_up, g_all):
+                gather.finish(q)
+            for side in range(2):
+
+                @pl.when(first + side != me_p)
+                def _():
+                    shuffle(q, side).wait_send()
+
+        g_half.finish(0)
+    for q in chunks:
+        with jax.named_scope("ch_add"):
+            t_child.add(q, own_ch.at[q])
+    result = own_ch[...].reshape(width, 2 * mk).T
+    for k in range(2):
+        child_out[k] = result[k * mk : (k + 1) * mk]
+    for q in chunks:
+        for scatter in (t_up, t_low, t_high, t_child):
+            scatter.finish(q)
+    t_piv.finish(0)
+
+
+def shards(panels, cols, *arguments):
+    *arrays, maps = arguments
+    m, width = arrays[1].shape
+    mk = arrays[0].shape[1]
+    wide = arrays[8].shape[2]
+    if panels != 2 * cols or mk % 128 or m % 256 or wide % 128 or width % (16 * SPLIT):
+        return plain_shards(panels, cols, *arguments)
+    wq = width // SPLIT
+    maps = maps.reshape(1, -1)
+    vm = pltpu.VMEM
+    dma = pltpu.SemaphoreType.DMA
+    return pl.pallas_call(
+        functools.partial(split_kernel, panels, cols),
+        out_shape=(
+            jax.ShapeDtypeStruct((m, width), F32),
+            jax.ShapeDtypeStruct((2, mk, width), F32),
+        ),
+        in_specs=[pl.BlockSpec(memory_space=pltpu.VMEM)] * 11,
+        out_specs=(pl.BlockSpec(memory_space=pltpu.VMEM),) * 2,
+        scratch_shapes=[
+            vm((2, SPLIT, wq, mk), BF),
+            vm((2, SPLIT, 2, cols, wq, mk), BF),
+            vm((SPLIT, 2, wq, m // 2), BF),
+            vm((SPLIT, 2, wq, m // 2), BF),
+            vm((2, m, m // 2), BF),
+            vm((3, SPLIT, wq, m), BF),
+            vm((3, SPLIT, 2, cols, wq, m), BF),
+            vm((width, 2 * mk), BF),
+            vm((2, cols, width, 2 * mk), BF),
+            vm((2, mk, 2 * m), BF),
+            vm((cols, width, 2 * mk), F32),
+            vm((SPLIT, cols - 1, wq, m), BF),
+            vm((SPLIT, cols - 1, wq, m), BF),
+            vm((cols - 1, width, 2 * mk), BF),
+            vm((cols - 1, width, 2 * mk), BF),
+            vm((2, SPLIT, cols - 1, wq, m), BF),
+            vm((2, SPLIT, cols - 1, wq, m), BF),
+            vm((SPLIT, cols - 1, wq, 2 * mk), BF),
+            vm((SPLIT, cols - 1, wq, 2 * mk), BF),
+            vm((SPLIT, wq, m), F32),
+            vm((width, 2 * mk), F32),
+            vm((2, SPLIT, wq, m), F32),
+            vm((SPLIT, wq, 2 * mk), F32),
+            vm((width, m), F32),
+            vm((width, m), F32),
+            dma((6, SPLIT, panels // 2)),
+            dma((6, SPLIT, cols, 2)),
+            dma((6, SPLIT, cols)),
+            dma((5, SPLIT, cols - 1)),
+            dma((5, SPLIT, cols - 1)),
+            dma((SPLIT, 2)),
+            dma((SPLIT, 2)),
+        ],
+        compiler_params=pltpu.CompilerParams(
+            collective_id=0, has_side_effects=True, vmem_limit_bytes=60 * 1024 * 1024
+        ),
+    )(*arrays, maps, maps)
+
+
 def solution(mesh):
     panels, cols = mesh.shape["panel"], mesh.shape["rhs"]
     placed = (

time: 108 us -> 95.2 us (0.88)
  the two profiles are of different devices: /device:TPU:24 before, /device:TPU:0 now
where the time goes in v1:
time: 95.2 us; the launch traced here: 95 us
  Pallas kernels  92 us (97%)
  local copies, waits for them, and re-layouts  2.42 us (3%)
    pallas_call x1, Pallas kernels, shards(): pl.pallas_call(functools.partial(split_kernel, panels, cols), out_shape=(...  92 us
    unnamed x4, local copies, waits for them, and re-layouts  2.42 us

profile of v1, /device:TPU:0, one launch (start us, length us, event | category | flops | bytes accessed | tf_op | source)
XLA Modules:
  0.0 95.0 jit_solution(15304667119104643113)
XLA Ops:
  0.6 92.0 %shard_map.113 = (f32[512,128]{1,0:T(8,128)}, f32[2,256,128]{2,1,0:T(8,128)}) custom-call(f32[2,256,128]{2,1,0:T(8,128)} %pivot_rhs.1, f32[512,128]{1,0:T(8,128)} %update_rhs.1, f32[512,128]{1,0:T(8,128)} %parent_rhs.1, bf16[2,256,512]{2,1,0:T(8,128)(2,1)} %lower_pivot.1, bf16[512,512]{1,0:T(8,128)(2,1)} %lower_update.1, bf16[512,1024]{1,0:T(8,128)(2,1)} %parent_lower.1, ...), custom_call_target="tpu_custom_call" | custom-call | tf_op jit(solution)/shard_map/pallas_call | solution.py:930
  92.6 0.0 copy-start
  92.6 1.7 %copy.14 = f32[512,128]{1,0:T(8,128)} copy(f32[512,128]{1,0:T(8,128)} %get-tuple-element.4) | data formatting | bytes 524288
  94.3 0.0 copy-done
  94.3 0.7 copy.15
Async XLA Ops:
  92.6 1.7 %copy-start = (f32[2,256,128]{2,1,0:T(8,128)S(1)}, f32[2,256,128]{2,1,0:T(8,128)}, u32[]{:S(2)}) copy-start(f32[2,256,128]{2,1,0:T(8,128)} %get-tuple-element.5) | copy-start | bytes 786436

commit v2 on v1

--- a/solution.py
+++ b/solution.py
@@ -464,17 +464,16 @@
 def split_kernel(
     panels,
     cols,
-    pivot_rhs,
-    update_rhs,
-    parent_rhs,
-    lower_pivot,
-    lower_update,
-    parent_lower,
-    parent_upper,
-    upper_pivot,
-    upper_update,
-    row_map,
-    col_map,
+    pivot_rhs_at,
+    update_rhs_at,
+    parent_rhs_at,
+    lower_pivot_at,
+    lower_update_at,
+    parent_lower_at,
+    parent_upper_at,
+    upper_pivot_at,
+    upper_update_at,
+    maps,
     parent_out,
     child_out,
     pin,
@@ -509,6 +508,16 @@
     rs_recv,
     sh_send,
     sh_recv,
+    pivot_rhs,
+    update_rhs,
+    parent_rhs,
+    lower_pivot,
+    lower_update,
+    parent_lower,
+    parent_upper,
+    upper_pivot,
+    upper_update,
+    in_sem,
 ):
     me_p, me_r = lax.axis_index("panel"), lax.axis_index("rhs")
     total = panels * cols
@@ -524,6 +533,22 @@
     last = cols - 1
     chunks = range(SPLIT)
 
+    arrays = (
+        (pivot_rhs_at, pivot_rhs),
+        (lower_update_at, lower_update),
+        (update_rhs_at, update_rhs),
+        (parent_rhs_at, parent_rhs),
+        (upper_update_at, upper_update),
+        (lower_pivot_at, lower_pivot),
+        (parent_lower_at, parent_lower),
+        (parent_upper_at, parent_upper),
+        (upper_pivot_at, upper_pivot),
+    )
+
+    def fetch(held):
+        index = [pair[1] is held for pair in arrays].index(True)
+        return pltpu.make_async_copy(*arrays[index], in_sem.at[index])
+
     barrier = pltpu.get_barrier_semaphore()
 
     @pl.loop(1, total)
@@ -536,6 +561,9 @@
             device_id_type=MESH,
         )
 
+    for _, held in arrays:
+        fetch(held).start()
+    fetch(pivot_rhs).wait()
     for k in range(2):
         turned = pivot_rhs[k].T.astype(BF)
         for q in chunks:
@@ -718,6 +746,9 @@
     for q in chunks:
         g_own.start(q)
 
+    fetch(update_rhs).wait()
+    fetch(parent_rhs).wait()
+    fetch(lower_update).wait()
     rhs_up[...] = update_rhs[...].T
     rhs_par[...] = parent_rhs[...].T
     own_par[...] = jnp.zeros_like(own_par)
@@ -725,7 +756,7 @@
     direct[...] = jnp.zeros_like(direct)
     rows = lax.broadcasted_iota(jnp.int32, (m, m // 2), 0)
     for k in range(2):
-        chosen[k] = (rows == targets(row_map, k, me_p, m // 2, me_p * m)).astype(F32).astype(BF)
+        chosen[k] = (rows == targets(maps, k, me_p, m // 2, me_p * m)).astype(F32).astype(BF)
 
     for q in chunks:
         with jax.named_scope("s1_pass"):
@@ -743,10 +774,11 @@
         g_other.start(q)
 
     wide = upper_update.shape[2]
+    fetch(upper_update).wait()
     with jax.named_scope("picked"):
         for k in range(2):
             rows = lax.broadcasted_iota(jnp.int32, (2 * m, wide), 0)
-            hot = (rows == targets(col_map, k, me_r, wide, me_r * 2 * m)).astype(F32).astype(BF)
+            hot = (rows == targets(maps, k, me_r, wide, me_r * 2 * m)).astype(F32).astype(BF)
             picked[k] = dot_rows(upper_update[k], hot).astype(BF)
 
     first = lax.rem(me_p, half) * 2
@@ -815,6 +847,7 @@
             if step < last:
                 t_piv.copy(0, step).start()
 
+    fetch(lower_pivot).wait()
     with jax.named_scope("pivots"):
         guard(g_other.active, pivots)
 
@@ -847,6 +880,7 @@
         with jax.named_scope(name + "_add"):
             combine(level, scatter, following, SPLIT - 1)
 
+    fetch(parent_lower).wait()
     parent(0, g_low, t_low, parent_lower, g_up, "low")
 
     with jax.named_scope("piv_add"):
@@ -854,8 +888,10 @@
     phalf[...] = own_piv[...].astype(BF)
     g_half.start(0)
 
+    fetch(parent_upper).wait()
     parent(1, g_up, t_high, parent_upper, g_all, "up")
 
+    fetch(upper_pivot).wait()
     with jax.named_scope("half_pass"):
         g_half.pass_on(0)
 
@@ -930,10 +966,10 @@
     return pl.pallas_call(
         functools.partial(split_kernel, panels, cols),
         out_shape=(
-            jax.ShapeDtypeStruct((m, width), F32),
-            jax.ShapeDtypeStruct((2, mk, width), F32),
+            pltpu.VMEM((m, width), F32),
+            pltpu.VMEM((2, mk, width), F32),
         ),
-        in_specs=[pl.BlockSpec(memory_space=pltpu.VMEM)] * 11,
+        in_specs=[pl.BlockSpec(memory_space=pl.ANY)] * 9 + [pl.BlockSpec(memory_space=pltpu.VMEM)],
         out_specs=(pl.BlockSpec(memory_space=pltpu.VMEM),) * 2,
         scratch_shapes=[
             vm((2, SPLIT, wq, mk), BF),
@@ -968,11 +1004,13 @@
             dma((5, SPLIT, cols - 1)),
             dma((SPLIT, 2)),
             dma((SPLIT, 2)),
+            *[vm(array.shape, array.dtype) for array in arrays],
+            dma((9,)),
         ],
         compiler_params=pltpu.CompilerParams(
             collective_id=0, has_side_effects=True, vmem_limit_bytes=60 * 1024 * 1024
         ),
-    )(*arrays, maps, maps)
+    )(*arrays, maps)
 
 
 def solution(mesh):

time: 95.2 us -> 91.9 us (0.965)
  Pallas kernels: 92 us -> 89.6 us
  local copies, waits for them, and re-layouts: 2.42 us -> 1.41 us
    pallas_call x1, Pallas kernels: 92 us -> 89.6 us  [shards(): pl.pallas_call(functools.partial(split_kernel, panels, cols), out_shape=(...]
    unnamed x4 -> x2, local copies, waits for them, and re-layouts: 2.42 us -> 1.41 us
where the time goes in v2:
time: 91.9 us; the launch traced here: 91.6 us
  Pallas kernels  89.6 us (97%)
  local copies, waits for them, and re-layouts  1.41 us (2%)
    pallas_call x1, Pallas kernels, shards(): pl.pallas_call(functools.partial(split_kernel, panels, cols), out_shape=(...  89.6 us

profile of v2, /device:TPU:0, one launch (start us, length us, event | category | flops | bytes accessed | tf_op | source)
XLA Modules:
  0.0 91.6 jit_solution(18114507695404151783)
XLA Ops:
  0.6 89.6 %shard_map.113 = (f32[512,128]{1,0:T(8,128)S(1)}, f32[2,256,128]{2,1,0:T(8,128)S(1)}) custom-call(f32[2,256,128]{2,1,0:T(8,128)} %pivot_rhs_at.1, f32[512,128]{1,0:T(8,128)} %update_rhs_at.1, f32[512,128]{1,0:T(8,128)} %parent_rhs_at.1, bf16[2,256,512]{2,1,0:T(8,128)(2,1)} %lower_pivot_at.1, bf16[512,512]{1,0:T(8,128)(2,1)} %lower_update_at.1, ...), custom_call_target="tpu_custom_call" | custom-call | tf_op jit(solution)/shard_map/pallas_call | solution.py:966
  90.2 0.7 copy.14
  90.9 0.7 copy.15

commit v3 on v2

--- a/solution.py
+++ b/solution.py
@@ -455,6 +455,8 @@
 
 
 SPLIT = 2
+LAG = 1
+FAR = (4,)
 
 
 def dot_rows(left, right):
@@ -597,7 +599,9 @@
             self.active = keep(me_r, group)
 
         def goal(self, step):
-            return lax.rem(group + step, half) * 2 + core
+            if self.stage in FAR:
+                return jnp.where(group < half // 2, half - 1 - step, step) * 2 + core
+            return lax.rem(group + 1 + step, half) * 2 + core
 
         def copy(self, q, step):
             goal = self.goal(step)
@@ -611,11 +615,10 @@
             )
 
         def sends(self, action):
-            for step in list(range(1, half)) + [0]:
-                condition = self.keep(group, self.goal(step) // 2)
-                if step == 0:
-                    condition = both(condition, group != me_r)
-                guard(condition, functools.partial(action, step))
+            for step in range(half):
+                goal = self.goal(step) // 2
+                elsewhere = jnp.logical_or(goal != group, group != me_r)
+                guard(both(self.keep(group, goal), elsewhere), functools.partial(action, step))
 
         def start(self, q):
             self.sends(lambda step: self.copy(q, step).start())
@@ -745,6 +748,8 @@
 
     for q in chunks:
         g_own.start(q)
+    for q in chunks:
+        g_other.start(q)
 
     fetch(update_rhs).wait()
     fetch(parent_rhs).wait()
@@ -757,70 +762,6 @@
     rows = lax.broadcasted_iota(jnp.int32, (m, m // 2), 0)
     for k in range(2):
         chosen[k] = (rows == targets(maps, k, me_p, m // 2, me_p * m)).astype(F32).astype(BF)
-
-    for q in chunks:
-        with jax.named_scope("s1_pass"):
-            g_own.pass_on(q)
-    for q in chunks:
-        with jax.named_scope("s1_arrive"):
-            g_own.arrive(q)
-        with jax.named_scope("s1_comp"):
-            value = sum(
-                dot_rows(gathered(x_pin[child, q, part]), lower_update[:, part * mk : (part + 1) * mk])
-                for part in range(2)
-            )
-            t_up.give(q, value, own_up.at[q])
-    for q in chunks:
-        g_other.start(q)
-
-    wide = upper_update.shape[2]
-    fetch(upper_update).wait()
-    with jax.named_scope("picked"):
-        for k in range(2):
-            rows = lax.broadcasted_iota(jnp.int32, (2 * m, wide), 0)
-            hot = (rows == targets(maps, k, me_r, wide, me_r * 2 * m)).astype(F32).astype(BF)
-            picked[k] = dot_rows(upper_update[k], hot).astype(BF)
-
-    first = lax.rem(me_p, half) * 2
-
-    def shuffle(q, side):
-        return pltpu.make_async_remote_copy(
-            src_ref=uhalf.at[q, side],
-            dst_ref=moved.at[q, child],
-            send_sem=sh_send.at[q, side],
-            recv_sem=sh_recv.at[q, child],
-            device_id=(first + side, me_r),
-            device_id_type=MESH,
-        )
-
-    for q in chunks:
-        own_up[q] += rhs_up[q * wq : (q + 1) * wq]
-        with jax.named_scope("s1_add"):
-            t_up.add(q, own_up.at[q])
-        update = own_up[q].astype(BF)
-        for side in range(2):
-            uhalf[q, side] = update[:, side * (m // 2) : (side + 1) * (m // 2)]
-
-            @pl.when(first + side != me_p)
-            def _():
-                shuffle(q, side).start()
-
-            @pl.when(first + side == me_p)
-            def _():
-                pltpu.make_async_copy(uhalf.at[q, side], moved.at[q, child], sh_recv.at[q, child]).start()
-
-    for q in chunks:
-        value = rhs_par[q * wq : (q + 1) * wq]
-        for k in range(2):
-            with jax.named_scope("moved"):
-                pltpu.make_async_copy(moved.at[q, k], moved.at[q, k], sh_recv.at[q, k]).wait()
-            value = value + dot_rows(moved[q, k], chosen[k])
-        vec[0, q] = value.astype(BF)
-        g_low.start(q)
-
-    for q in chunks:
-        with jax.named_scope("other_pass"):
-            g_other.pass_on(q)
 
     def pivots():
         for q in chunks:
@@ -847,9 +788,77 @@
             if step < last:
                 t_piv.copy(0, step).start()
 
+    for q in chunks:
+        with jax.named_scope("s1_pass"):
+            g_own.pass_on(q)
+    for q in chunks:
+        with jax.named_scope("s1_arrive"):
+            g_own.arrive(q)
+        with jax.named_scope("s1_comp"):
+            value = sum(
+                dot_rows(gathered(x_pin[child, q, part]), lower_update[:, part * mk : (part + 1) * mk])
+                for part in range(2)
+            )
+            t_up.give(q, value, own_up.at[q])
+    for q in chunks:
+        with jax.named_scope("other_pass"):
+            g_other.pass_on(q)
+
     fetch(lower_pivot).wait()
     with jax.named_scope("pivots"):
         guard(g_other.active, pivots)
+
+
+    wide = upper_update.shape[2]
+    fetch(upper_update).wait()
+    with jax.named_scope("picked"):
+        for k in range(2):
+            rows = lax.broadcasted_iota(jnp.int32, (2 * m, wide), 0)
+            hot = (rows == targets(maps, k, me_r, wide, me_r * 2 * m)).astype(F32).astype(BF)
+            picked[k] = dot_rows(upper_update[k], hot).astype(BF)
+
+    first = lax.rem(me_p, half) * 2
+
+    def shuffle(q, side):
+        return pltpu.make_async_remote_copy(
+            src_ref=uhalf.at[q, side],
+            dst_ref=moved.at[q, child],
+            send_sem=sh_send.at[q, side],
+            recv_sem=sh_recv.at[q, child],
+            device_id=(first + side, me_r),
+            device_id_type=MESH,
+        )
+
+    def reduce(q):
+        own_up[q] += rhs_up[q * wq : (q + 1) * wq]
+        with jax.named_scope("s1_add"):
+            t_up.add(q, own_up.at[q])
+        update = own_up[q].astype(BF)
+        for side in range(2):
+            uhalf[q, side] = update[:, side * (m // 2) : (side + 1) * (m // 2)]
+
+            @pl.when(first + side != me_p)
+            def _():
+                shuffle(q, side).start()
+
+            @pl.when(first + side == me_p)
+            def _():
+                pltpu.make_async_copy(uhalf.at[q, side], moved.at[q, child], sh_recv.at[q, child]).start()
+
+    def assemble(q):
+        value = rhs_par[q * wq : (q + 1) * wq]
+        for k in range(2):
+            with jax.named_scope("moved"):
+                pltpu.make_async_copy(moved.at[q, k], moved.at[q, k], sh_recv.at[q, k]).wait()
+            value = value + dot_rows(moved[q, k], chosen[k])
+        vec[0, q] = value.astype(BF)
+        g_low.start(q)
+
+    for q in chunks:
+        reduce(q)
+        if q >= 1:
+            assemble(q - 1)
+    assemble(SPLIT - 1)
 
     def multiply(level, gather, scatter, factor, q):
         def action():
@@ -868,28 +877,45 @@
         vec[level + 1, q] = own_par[level, q].astype(BF)
         following.start(q)
 
-    def parent(level, gather, scatter, factor, following, name):
+    def parent(level, gather, scatter, factor, following, name, extra, between):
+        def settle(q):
+            with jax.named_scope(name + "_add"):
+                combine(level, scatter, following, q)
+
         for q in chunks:
             with jax.named_scope(name + "_pass"):
                 gather.pass_on(q)
-            if q:
-                with jax.named_scope(name + "_add"):
-                    combine(level, scatter, following, q - 1)
             with jax.named_scope(name + "_mul"):
                 multiply(level, gather, scatter, factor, q)
-        with jax.named_scope(name + "_add"):
-            combine(level, scatter, following, SPLIT - 1)
+            if q == SPLIT - 1:
+                extra()
+            if q == LAG - 1:
+                between()
+            if q >= LAG - 1:
+                settle(q - LAG + 1)
+        for q in range(SPLIT - LAG + 1, SPLIT):
+            settle(q)
+
+    def nothing():
+        return None
+
+    def start_other():
+        for q in chunks:
+            g_other.start(q)
+
+    def start_half():
+        with jax.named_scope("piv_add"):
+            t_piv.add(0, own_piv)
+        phalf[...] = own_piv[...].astype(BF)
+        g_half.start(0)
 
     fetch(parent_lower).wait()
-    parent(0, g_low, t_low, parent_lower, g_up, "low")
-
-    with jax.named_scope("piv_add"):
-        t_piv.add(0, own_piv)
-    phalf[...] = own_piv[...].astype(BF)
-    g_half.start(0)
+    parent(0, g_low, t_low, parent_lower, g_up, "low", nothing, nothing)
+
+    start_half()
 
     fetch(parent_upper).wait()
-    parent(1, g_up, t_high, parent_upper, g_all, "up")
+    parent(1, g_up, t_high, parent_upper, g_all, "up", nothing, nothing)
 
     fetch(upper_pivot).wait()
     with jax.named_scope("half_pass"):
@@ -909,6 +935,7 @@
 
     with jax.named_scope("known"):
         guard(g_half.active, known)
+
     parent_out[...] = own_par[1].reshape(width, m).T
 
     for q in chunks:

time: 91.9 us -> 88.5 us (0.963)
  Pallas kernels: 89.6 us -> 85.9 us
    pallas_call x1, Pallas kernels: 89.6 us -> 85.9 us  [shards(): pl.pallas_call(functools.partial(split_kernel, panels, cols), out_shape=(...]
where the time goes in v3:
time: 88.5 us; the launch traced here: 88 us
  Pallas kernels  85.9 us (97%)
  local copies, waits for them, and re-layouts  1.41 us (2%)
    pallas_call x1, Pallas kernels, shards(): pl.pallas_call(functools.partial(split_kernel, panels, cols), out_shape=(...  85.9 us

profile of v3, /device:TPU:0, one launch (start us, length us, event | category | flops | bytes accessed | tf_op | source)
XLA Modules:
  0.0 88.0 jit_solution(1510878551616360715)
XLA Ops:
  0.6 85.9 %shard_map.113 = (f32[512,128]{1,0:T(8,128)S(1)}, f32[2,256,128]{2,1,0:T(8,128)S(1)}) custom-call(f32[2,256,128]{2,1,0:T(8,128)} %pivot_rhs_at.1, f32[512,128]{1,0:T(8,128)} %update_rhs_at.1, f32[512,128]{1,0:T(8,128)} %parent_rhs_at.1, bf16[2,256,512]{2,1,0:T(8,128)(2,1)} %lower_pivot_at.1, bf16[512,512]{1,0:T(8,128)(2,1)} %lower_update_at.1, ...), custom_call_target="tpu_custom_call" | custom-call | tf_op jit(solution)/shard_map/pallas_call | solution.py:993
  86.6 0.7 copy.14
  87.3 0.7 copy.15

commit v4 on v0

--- a/solution.py
+++ b/solution.py
@@ -16,7 +16,7 @@
     return jnp.dot(left, right, preferred_element_type=F32)
 
 
-def kernel(
+def plain_kernel(
     panels,
     cols,
     pivot_rhs,
@@ -392,7 +392,7 @@
         scatter.finish()
 
 
-def shards(panels, cols, *arguments):
+def plain_shards(panels, cols, *arguments):
     *arrays, maps = arguments
     m, width = arrays[1].shape
     mk = arrays[0].shape[1]
@@ -411,7 +411,7 @@
     vm = pltpu.VMEM
     dma = pltpu.SemaphoreType.DMA
     return pl.pallas_call(
-        functools.partial(kernel, panels, cols),
+        functools.partial(plain_kernel, panels, cols),
         out_shape=(
             jax.ShapeDtypeStruct((m, width), F32),
             jax.ShapeDtypeStruct((2, mk, width), F32),
@@ -454,6 +454,565 @@
     )(*arrays, row_map, col_map)
 
 
+SPLIT = 2
+FAR = (4,)
+
+
+def dot_rows(left, right):
+    return lax.dot_general(left, right, (((1,), (1,)), ((), ())), preferred_element_type=F32)
+
+
+def split_kernel(
+    panels,
+    cols,
+    pivot_at,
+    update_at,
+    parent_at,
+    lower_pivot_at,
+    lower_update_at,
+    parent_lower_at,
+    parent_upper_at,
+    upper_pivot_at,
+    upper_update_at,
+    maps,
+    parent_out,
+    child_out,
+    pivot_rhs,
+    update_rhs,
+    parent_rhs,
+    lower_pivot,
+    lower_update,
+    parent_lower,
+    parent_upper,
+    upper_pivot,
+    upper_update,
+    pin,
+    x_pin,
+    uhalf,
+    moved,
+    chosen,
+    vec,
+    x_par,
+    phalf,
+    x_half,
+    picked,
+    direct,
+    s_par,
+    r_par,
+    s_piv,
+    r_piv,
+    own_par,
+    own_piv,
+    sum_par,
+    sum_piv,
+    g_send,
+    g_recv,
+    rs_send,
+    rs_recv,
+    sh_send,
+    sh_recv,
+    in_sem,
+    mate_send,
+    mate_recv,
+):
+    me_p, me_r = lax.axis_index("panel"), lax.axis_index("rhs")
+    total = panels * cols
+    me = me_p * cols + me_r
+    core = lax.rem(me_p, 2)
+    mate = me_p + 1 - 2 * core
+    half = panels // 2
+    m, width = parent_rhs.shape
+    mk = pivot_rhs.shape[1]
+    wq = width // SPLIT
+    wj = wq // 2
+    child = me_p // half
+    group = me_p // 2
+    last = cols - 1
+    chunks = range(SPLIT)
+
+    factors = (
+        (lower_update_at, lower_update),
+        (lower_pivot_at, lower_pivot),
+        (upper_update_at, upper_update),
+        (parent_lower_at, parent_lower),
+        (parent_upper_at, parent_upper),
+        (upper_pivot_at, upper_pivot),
+    )
+    vectors = ((pivot_at, pivot_rhs), (update_at, update_rhs), (parent_at, parent_rhs))
+
+    def own_rows(index):
+        return pltpu.make_async_copy(factors[index][0], factors[index][1].at[core], in_sem.at[index])
+
+    def mate_rows(index):
+        return pltpu.make_async_remote_copy(
+            src_ref=factors[index][0],
+            dst_ref=factors[index][1].at[core],
+            send_sem=mate_send.at[index],
+            recv_sem=mate_recv.at[index],
+            device_id=(mate, me_r),
+            device_id_type=MESH,
+        )
+
+    def ready(held):
+        index = [pair[1] is held for pair in factors].index(True)
+        own_rows(index).wait()
+        place = held.at[1 - core]
+        pltpu.make_async_copy(place, place, mate_recv.at[index]).wait()
+
+    def fetch(index):
+        return pltpu.make_async_copy(*vectors[index], in_sem.at[6 + index])
+
+    fetch(0).start()
+    barrier = pltpu.get_barrier_semaphore()
+
+    @pl.loop(1, total)
+    def _(step):
+        other = lax.rem(me + step, total)
+        pl.semaphore_signal(
+            barrier,
+            inc=1,
+            device_id=(other // cols, lax.rem(other, cols)),
+            device_id_type=MESH,
+        )
+
+    own_rows(0).start()
+    fetch(1).start()
+    fetch(2).start()
+    for index in range(1, 6):
+        own_rows(index).start()
+    fetch(0).wait()
+    for k in range(2):
+        pin[k] = pivot_rhs[k].T.astype(BF).reshape(SPLIT, 2, wj, mk)
+    with jax.named_scope("barrier"):
+        pl.semaphore_wait(barrier, total - 1)
+
+    def every(source, goal):
+        return None
+
+    def below(source, goal):
+        return goal >= source
+
+    def above(source, goal):
+        return goal <= source
+
+    def guard(condition, action):
+        if condition is None:
+            action()
+        else:
+            pl.when(condition)(action)
+
+    def both(first, second):
+        return second if first is None else jnp.logical_and(first, second)
+
+    sent_place = lax.rem(me_r - group - 1 + 2 * cols, cols)
+
+    class Gather:
+        def __init__(self, stage, piece, place, keep):
+            self.stage, self.piece, self.place, self.keep = stage, piece, place, keep
+            self.active = keep(me_r, group)
+
+        def plane(self, step):
+            if self.stage in FAR:
+                return jnp.where(group < half // 2, half - 1 - step, step)
+            return lax.rem(group + 1 + step, half)
+
+        def copy(self, q, step, side):
+            goal = self.plane(step) * 2 + side
+            return pltpu.make_async_remote_copy(
+                src_ref=self.piece(q, side, goal),
+                dst_ref=self.place(q, core, sent_place, goal),
+                send_sem=g_send.at[self.stage, q, side, step],
+                recv_sem=g_recv.at[self.stage, q, sent_place, core],
+                device_id=(goal, group),
+                device_id_type=MESH,
+            )
+
+        def sends(self, action):
+            for step in range(half):
+                goal = self.plane(step)
+                for side in range(2):
+                    elsewhere = jnp.logical_or(goal != group, group != me_r)
+                    elsewhere = jnp.logical_or(elsewhere, core != side)
+                    guard(both(self.keep(group, goal), elsewhere), functools.partial(action, step, side))
+
+        def start(self, q):
+            self.sends(lambda step, side: self.copy(q, step, side).start())
+
+            @pl.when(group == me_r)
+            def _():
+                pltpu.make_async_copy(
+                    self.piece(q, core, me_p),
+                    self.place(q, core, last, me_p),
+                    g_recv.at[self.stage, q, last, core],
+                ).start()
+
+        def arrive(self, q):
+            for spot in [last] + list(range(last)):
+                for part in range(2):
+                    place = self.place(q, part, spot, me_p)
+                    pltpu.make_async_copy(place, place, g_recv.at[self.stage, q, spot, part]).wait()
+
+        def finish(self, q):
+            self.sends(lambda step, side: self.copy(q, step, side).wait_send())
+
+    class Scatter:
+        def __init__(self, stage, source, target, own, keep):
+            self.stage, self.source, self.target, self.own, self.keep = stage, source, target, own, keep
+            self.active = keep(me_r, group)
+
+        def copy(self, q, step, side):
+            return pltpu.make_async_remote_copy(
+                src_ref=self.source.at[q, step, side],
+                dst_ref=self.target.at[q, core, step],
+                send_sem=rs_send.at[self.stage, q, step, side],
+                recv_sem=rs_recv.at[self.stage, q, core, step],
+                device_id=(group * 2 + side, lax.rem(me_r + 1 + step, cols)),
+                device_id_type=MESH,
+            )
+
+        def to_mate(self, q):
+            return pltpu.make_async_remote_copy(
+                src_ref=self.source.at[q, last, 1 - core],
+                dst_ref=self.target.at[q, core, last],
+                send_sem=rs_send.at[self.stage, q, last, 0],
+                recv_sem=rs_recv.at[self.stage, q, core, last],
+                device_id=(mate, me_r),
+                device_id_type=MESH,
+            )
+
+        def put(self, q, side, lanes, value):
+            for step in range(cols):
+                block = value[step * wj : (step + 1) * wj]
+                self.source[q, step, side, :, lanes] = block.astype(BF)
+            self.own[q, side, :, lanes] = value[last * wj :]
+
+        def start(self, q):
+            for step in range(last):
+                for side in range(2):
+                    self.copy(q, step, side).start()
+            self.to_mate(q).start()
+
+        def landed(self, q, side, step):
+            place = self.target.at[q, side, step]
+            pltpu.make_async_copy(place, place, rs_recv.at[self.stage, q, side, step]).wait()
+
+        def add(self, q, total_ref):
+            def mine():
+                total_ref[core] += self.own[q, core]
+                self.landed(q, 1 - core, last)
+                total_ref[1 - core] += self.target[q, 1 - core, last].astype(F32)
+
+            guard(self.active, mine)
+            for step in range(last):
+                sender = lax.rem(me_r + last - step, cols)
+
+                def action(step=step):
+                    for side in range(2):
+                        self.landed(q, side, step)
+                        total_ref[side] += self.target[q, side, step].astype(F32)
+
+                guard(self.keep(sender, group), action)
+
+        def finish(self, q):
+            def action():
+                for step in range(last):
+                    for side in range(2):
+                        self.copy(q, step, side).wait_send()
+                self.to_mate(q).wait_send()
+
+            guard(self.active, action)
+
+    def same(panel):
+        return panel // half
+
+    def other(panel):
+        return 1 - panel // half
+
+    def pins(pick):
+        return (
+            lambda q, side, goal: pin.at[pick(goal), q, side],
+            lambda q, part, spot, goal: x_pin.at[pick(goal), q, part, spot],
+        )
+
+    def level_parts(level):
+        return (
+            lambda q, side, goal: vec.at[level, q, side],
+            lambda q, part, spot, goal: x_par.at[level, q, part, spot],
+        )
+
+    g_own = Gather(0, *pins(same), every)
+    g_other = Gather(5, *pins(other), below)
+    g_low = Gather(1, *level_parts(0), below)
+    g_up = Gather(3, *level_parts(1), above)
+    g_all = Gather(4, *level_parts(2), every)
+    g_half = Gather(
+        2,
+        lambda q, side, goal: phalf.at[q, side],
+        lambda q, part, spot, goal: x_half.at[q, part, spot],
+        above,
+    )
+    t_up, t_low, t_high = [
+        Scatter(stage, s_par.at[stage], r_par.at[stage], own_par.at[stage], keep)
+        for stage, keep in enumerate((every, below, above))
+    ]
+    t_piv, t_child = [
+        Scatter(3 + index, s_piv.at[index], r_piv.at[index], own_piv.at[index], keep)
+        for index, keep in enumerate((below, every))
+    ]
+
+    def gathered(block):
+        return block.reshape(cols * block.shape[1], block.shape[2])
+
+    for q in chunks:
+        g_own.start(q)
+    for index in range(6):
+        mate_rows(index).start()
+    for q in chunks:
+        g_other.start(q)
+
+    fetch(1).wait()
+    fetch(2).wait()
+    sum_par[0] = update_rhs[...].T.reshape(SPLIT, 2, wj, m)
+    sum_par[3] = parent_rhs[...].T.reshape(SPLIT, 2, wj, m)
+    for level in (1, 2):
+        sum_par[level] = jnp.zeros_like(sum_par[level])
+    sum_piv[...] = jnp.zeros_like(sum_piv)
+    direct[...] = jnp.zeros_like(direct)
+    rows = lax.broadcasted_iota(jnp.int32, (m, m // 2), 0)
+    for k in range(2):
+        start = pl.multiple_of(k * (maps.shape[1] // 2) + me_p * (m // 2), 128)
+        chosen[k] = (rows == maps[:, pl.ds(start, m // 2)] - me_p * m).astype(F32).astype(BF)
+    ready(lower_update)
+
+    def spread(scatter, q, value, size):
+        for side in range(2):
+            scatter.put(q, side, slice(None), value[:, side * size : (side + 1) * size])
+        scatter.start(q)
+
+    for q in chunks:
+        with jax.named_scope("s1_arrive"):
+            g_own.arrive(q)
+        with jax.named_scope("s1_comp"):
+            held = lower_update[...].reshape(2 * m, 2 * mk)
+            value = sum(
+                dot_rows(gathered(x_pin[child, q, part]), held[:, part * mk : (part + 1) * mk])
+                for part in range(2)
+            )
+            spread(t_up, q, value, m)
+
+    ready(lower_pivot)
+
+    def pivots():
+        for q in chunks:
+            g_other.arrive(q)
+            for side in range(2):
+                for k in range(2):
+                    value = sum(
+                        dot_rows(
+                            gathered(x_pin[k, q, part]),
+                            lower_pivot[side, k, :, part * mk : (part + 1) * mk],
+                        )
+                        for part in range(2)
+                    )
+                    t_piv.put(q, side, slice(k * mk, (k + 1) * mk), value)
+            t_piv.start(q)
+
+    with jax.named_scope("pivots"):
+        guard(g_other.active, pivots)
+
+    wide = upper_update.shape[3]
+    ready(upper_update)
+    with jax.named_scope("picked"):
+        rows = lax.broadcasted_iota(jnp.int32, (2 * m, wide), 0)
+        for k in range(2):
+            start = pl.multiple_of(k * (maps.shape[1] // 2) + me_r * wide, 128)
+            hot = (rows == maps[:, pl.ds(start, wide)] - me_r * 2 * m).astype(F32).astype(BF)
+            for side in range(2):
+                picked[side, k] = dot_rows(upper_update[side, k], hot).astype(BF)
+
+    first = lax.rem(me_p, half) * 2
+
+    def shuffle(q, side):
+        return pltpu.make_async_remote_copy(
+            src_ref=uhalf.at[q, side],
+            dst_ref=moved.at[q, child],
+            send_sem=sh_send.at[q, side],
+            recv_sem=sh_recv.at[q, child],
+            device_id=(first + side, me_r),
+            device_id_type=MESH,
+        )
+
+    def reduce(q):
+        with jax.named_scope("s1_add"):
+            t_up.add(q, sum_par.at[0, q])
+        update = sum_par[0, q].reshape(wq, m).astype(BF)
+        for side in range(2):
+            uhalf[q, side] = update[:, side * (m // 2) : (side + 1) * (m // 2)]
+
+            @pl.when(first + side != me_p)
+            def _():
+                shuffle(q, side).start()
+
+            @pl.when(first + side == me_p)
+            def _():
+                pltpu.make_async_copy(uhalf.at[q, side], moved.at[q, child], sh_recv.at[q, child]).start()
+
+    def assemble(q):
+        value = sum_par[3, q].reshape(wq, m)
+        for k in range(2):
+            with jax.named_scope("moved"):
+                pltpu.make_async_copy(moved.at[q, k], moved.at[q, k], sh_recv.at[q, k]).wait()
+            value = value + dot_rows(moved[q, k], chosen[k])
+        vec[0, q] = value.astype(BF).reshape(2, wj, m)
+        g_low.start(q)
+
+    for q in chunks:
+        reduce(q)
+        if q >= 1:
+            assemble(q - 1)
+    assemble(SPLIT - 1)
+
+    def parent(level, gather, scatter, factor, following, name):
+        ready(factor)
+        for q in chunks:
+
+            def action(q=q):
+                with jax.named_scope(name + "_arrive"):
+                    gather.arrive(q)
+                held = factor[...].reshape(2 * m, 2 * m)
+                value = sum(
+                    dot_rows(gathered(x_par[level, q, part]), held[:, part * m : (part + 1) * m])
+                    for part in range(2)
+                )
+                spread(scatter, q, value, m)
+
+            guard(gather.active, action)
+            with jax.named_scope(name + "_add"):
+                scatter.add(q, sum_par.at[level + 1, q])
+            vec[level + 1, q] = sum_par[level + 1, q].astype(BF)
+            following.start(q)
+
+    parent(0, g_low, t_low, parent_lower, g_up, "low")
+
+    for q in chunks:
+        with jax.named_scope("piv_add"):
+            t_piv.add(q, sum_piv.at[0, q])
+        phalf[q] = sum_piv[0, q].astype(BF)
+        g_half.start(q)
+
+    parent(1, g_up, t_high, parent_upper, g_all, "up")
+
+    ready(upper_pivot)
+
+    def known():
+        for q in chunks:
+            g_half.arrive(q)
+            for side in range(2):
+                for k in range(2):
+                    value = sum(
+                        dot_rows(
+                            gathered(x_half[q, part, :, :, k * mk : (k + 1) * mk]),
+                            upper_pivot[side, k, :, part * mk : (part + 1) * mk],
+                        )
+                        for part in range(2)
+                    )
+                    base = (side * 2 + k) * mk
+                    direct[q, :, base : base + mk] = value
+
+    with jax.named_scope("known"):
+        guard(g_half.active, known)
+    parent_out[...] = sum_par[2].reshape(width, m).T
+
+    for q in chunks:
+        with jax.named_scope("all_arrive"):
+            g_all.arrive(q)
+        with jax.named_scope("all_comp"):
+            held = picked[...].reshape(4 * mk, 2 * m)
+            value = direct[q] + sum(
+                dot_rows(gathered(x_par[2, q, part]), held[:, part * m : (part + 1) * m])
+                for part in range(2)
+            )
+            spread(t_child, q, value, 2 * mk)
+
+    with jax.named_scope("gfinish"):
+        for index in range(6):
+            mate_rows(index).wait_send()
+        for q in chunks:
+            for gather in (g_own, g_other, g_low, g_half, g_up, g_all):
+                gather.finish(q)
+            for side in range(2):
+
+                @pl.when(first + side != me_p)
+                def _():
+                    shuffle(q, side).wait_send()
+
+    for q in chunks:
+        with jax.named_scope("ch_add"):
+            t_child.add(q, sum_piv.at[1, q])
+    result = sum_piv[1].reshape(width, 2 * mk).T
+    for k in range(2):
+        child_out[k] = result[k * mk : (k + 1) * mk]
+    for q in chunks:
+        for scatter in (t_up, t_low, t_high, t_piv, t_child):
+            scatter.finish(q)
+
+
+def shards(panels, cols, *arguments):
+    *arrays, maps = arguments
+    m, width = arrays[1].shape
+    mk = arrays[0].shape[1]
+    wide = arrays[8].shape[2]
+    if panels != 2 * cols or mk % 128 or m != 2 * mk or m % 256 or wide % 128 or width % (32 * SPLIT):
+        return plain_shards(panels, cols, *arguments)
+    wj = width // SPLIT // 2
+    vm = pltpu.VMEM
+    dma = pltpu.SemaphoreType.DMA
+    return pl.pallas_call(
+        functools.partial(split_kernel, panels, cols),
+        out_shape=(
+            pltpu.VMEM((m, width), F32),
+            pltpu.VMEM((2, mk, width), F32),
+        ),
+        in_specs=[pl.BlockSpec(memory_space=pl.ANY)] * 9 + [pl.BlockSpec(memory_space=pltpu.VMEM)],
+        out_specs=(pl.BlockSpec(memory_space=pltpu.VMEM),) * 2,
+        scratch_shapes=[
+            *[vm(array.shape, array.dtype) for array in arrays[:3]],
+            *[vm((2,) + array.shape, array.dtype) for array in arrays[3:]],
+            vm((2, SPLIT, 2, wj, mk), BF),
+            vm((2, SPLIT, 2, cols, wj, mk), BF),
+            vm((SPLIT, 2, 2 * wj, m // 2), BF),
+            vm((SPLIT, 2, 2 * wj, m // 2), BF),
+            vm((2, m, m // 2), BF),
+            vm((3, SPLIT, 2, wj, m), BF),
+            vm((3, SPLIT, 2, cols, wj, m), BF),
+            vm((SPLIT, 2, wj, 2 * mk), BF),
+            vm((SPLIT, 2, cols, wj, 2 * mk), BF),
+            vm((2, 2, mk, 2 * m), BF),
+            vm((SPLIT, cols * wj, 4 * mk), F32),
+            vm((3, SPLIT, cols, 2, wj, m), BF),
+            vm((3, SPLIT, 2, cols, wj, m), BF),
+            vm((2, SPLIT, cols, 2, wj, 2 * mk), BF),
+            vm((2, SPLIT, 2, cols, wj, 2 * mk), BF),
+            vm((3, SPLIT, 2, wj, m), F32),
+            vm((2, SPLIT, 2, wj, 2 * mk), F32),
+            vm((4, SPLIT, 2, wj, m), F32),
+            vm((2, SPLIT, 2, wj, 2 * mk), F32),
+            dma((6, SPLIT, 2, panels // 2)),
+            dma((6, SPLIT, cols, 2)),
+            dma((5, SPLIT, cols, 2)),
+            dma((5, SPLIT, 2, cols)),
+            dma((SPLIT, 2)),
+            dma((SPLIT, 2)),
+            dma((9,)),
+            dma((6,)),
+            dma((6,)),
+        ],
+        compiler_params=pltpu.CompilerParams(
+            collective_id=0, has_side_effects=True, vmem_limit_bytes=60 * 1024 * 1024
+        ),
+    )(*arrays, maps.reshape(1, -1))
+
+
 def solution(mesh):
     panels, cols = mesh.shape["panel"], mesh.shape["rhs"]
     placed = (

time: 108 us -> 85.6 us (0.79)
  the two profiles are of different devices: /device:TPU:24 before, /device:TPU:0 now
where the time goes in v4:
time: 85.6 us; the launch traced here: 84.5 us
  Pallas kernels  82.5 us (96%)
  local copies, waits for them, and re-layouts  1.41 us (2%)
    pallas_call x1, Pallas kernels, shards(): pl.pallas_call(functools.partial(split_kernel, panels, cols), out_shape=(...  82.5 us

profile of v4, /device:TPU:0, one launch (start us, length us, event | category | flops | bytes accessed | tf_op | source)
XLA Modules:
  0.0 84.5 jit_solution(12339968879384162663)
XLA Ops:
  0.6 82.5 %shard_map.113 = (f32[512,128]{1,0:T(8,128)S(1)}, f32[2,256,128]{2,1,0:T(8,128)S(1)}) custom-call(f32[2,256,128]{2,1,0:T(8,128)} %pivot_at.1, f32[512,128]{1,0:T(8,128)} %update_at.1, f32[512,128]{1,0:T(8,128)} %parent_at.1, bf16[2,256,512]{2,1,0:T(8,128)(2,1)} %lower_pivot_at.1, bf16[512,512]{1,0:T(8,128)(2,1)} %lower_update_at.1, ...), custom_call_target="tpu_custom_call" | custom-call | tf_op jit(solution)/shard_map/pallas_call | solution.py:970
  83.1 0.7 copy.14
  83.8 0.7 copy.15

commit v5 on v4

--- a/solution.py
+++ b/solution.py
@@ -800,8 +800,6 @@
             )
             spread(t_up, q, value, m)
 
-    ready(lower_pivot)
-
     def pivots():
         for q in chunks:
             g_other.arrive(q)
@@ -817,9 +815,50 @@
                     t_piv.put(q, side, slice(k * mk, (k + 1) * mk), value)
             t_piv.start(q)
 
+    ready(lower_pivot)
     with jax.named_scope("pivots"):
         guard(g_other.active, pivots)
 
+    first = lax.rem(me_p, half) * 2
+
+    def shuffle(q, side):
+        return pltpu.make_async_remote_copy(
+            src_ref=uhalf.at[q, side],
+            dst_ref=moved.at[q, child],
+            send_sem=sh_send.at[q, side],
+            recv_sem=sh_recv.at[q, child],
+            device_id=(first + side, me_r),
+            device_id_type=MESH,
+        )
+
+    def reduce(q):
+        with jax.named_scope("s1_add"):
+            t_up.add(q, sum_par.at[0, q])
+        update = sum_par[0, q].reshape(wq, m).astype(BF)
+        for side in range(2):
+            uhalf[q, side] = update[:, side * (m // 2) : (side + 1) * (m // 2)]
+
+            @pl.when(first + side != me_p)
+            def _():
+                shuffle(q, side).start()
+
+            @pl.when(first + side == me_p)
+            def _():
+                pltpu.make_async_copy(uhalf.at[q, side], moved.at[q, child], sh_recv.at[q, child]).start()
+
+    def assemble(q):
+        value = sum_par[3, q].reshape(wq, m)
+        for k in range(2):
+            with jax.named_scope("moved"):
+                pltpu.make_async_copy(moved.at[q, k], moved.at[q, k], sh_recv.at[q, k]).wait()
+            value = value + dot_rows(moved[q, k], chosen[k])
+        vec[0, q] = value.astype(BF).reshape(2, wj, m)
+        g_low.start(q)
+
+    reduce(0)
+    reduce(1)
+    assemble(0)
+    assemble(1)
     wide = upper_update.shape[3]
     ready(upper_update)
     with jax.named_scope("picked"):
@@ -830,47 +869,6 @@
             for side in range(2):
                 picked[side, k] = dot_rows(upper_update[side, k], hot).astype(BF)
 
-    first = lax.rem(me_p, half) * 2
-
-    def shuffle(q, side):
-        return pltpu.make_async_remote_copy(
-            src_ref=uhalf.at[q, side],
-            dst_ref=moved.at[q, child],
-            send_sem=sh_send.at[q, side],
-            recv_sem=sh_recv.at[q, child],
-            device_id=(first + side, me_r),
-            device_id_type=MESH,
-        )
-
-    def reduce(q):
-        with jax.named_scope("s1_add"):
-            t_up.add(q, sum_par.at[0, q])
-        update = sum_par[0, q].reshape(wq, m).astype(BF)
-        for side in range(2):
-            uhalf[q, side] = update[:, side * (m // 2) : (side + 1) * (m // 2)]
-
-            @pl.when(first + side != me_p)
-            def _():
-                shuffle(q, side).start()
-
-            @pl.when(first + side == me_p)
-            def _():
-                pltpu.make_async_copy(uhalf.at[q, side], moved.at[q, child], sh_recv.at[q, child]).start()
-
-    def assemble(q):
-        value = sum_par[3, q].reshape(wq, m)
-        for k in range(2):
-            with jax.named_scope("moved"):
-                pltpu.make_async_copy(moved.at[q, k], moved.at[q, k], sh_recv.at[q, k]).wait()
-            value = value + dot_rows(moved[q, k], chosen[k])
-        vec[0, q] = value.astype(BF).reshape(2, wj, m)
-        g_low.start(q)
-
-    for q in chunks:
-        reduce(q)
-        if q >= 1:
-            assemble(q - 1)
-    assemble(SPLIT - 1)
 
     def parent(level, gather, scatter, factor, following, name):
         ready(factor)
@@ -892,13 +890,13 @@
             vec[level + 1, q] = sum_par[level + 1, q].astype(BF)
             following.start(q)
 
-    parent(0, g_low, t_low, parent_lower, g_up, "low")
-
     for q in chunks:
         with jax.named_scope("piv_add"):
             t_piv.add(q, sum_piv.at[0, q])
         phalf[q] = sum_piv[0, q].astype(BF)
         g_half.start(q)
+
+    parent(0, g_low, t_low, parent_lower, g_up, "low")
 
     parent(1, g_up, t_high, parent_upper, g_all, "up")
 

time: 85.6 us -> 80.5 us (0.940)
  Pallas kernels: 82.5 us -> 77.8 us
    pallas_call x1, Pallas kernels: 82.5 us -> 77.8 us  [shards(): pl.pallas_call(functools.partial(split_kernel, panels, cols), out_shape=(...]
where the time goes in v5:
time: 80.5 us; the launch traced here: 79.8 us
  Pallas kernels  77.8 us (97%)
  local copies, waits for them, and re-layouts  1.41 us (2%)
    pallas_call x1, Pallas kernels, shards(): pl.pallas_call(functools.partial(split_kernel, panels, cols), out_shape=(...  77.8 us

profile of v5, /device:TPU:0, one launch (start us, length us, event | category | flops | bytes accessed | tf_op | source)
XLA Modules:
  0.0 79.8 jit_solution(12059198148961389931)
XLA Ops:
  0.6 77.8 %shard_map.113 = (f32[512,128]{1,0:T(8,128)S(1)}, f32[2,256,128]{2,1,0:T(8,128)S(1)}) custom-call(f32[2,256,128]{2,1,0:T(8,128)} %pivot_at.1, f32[512,128]{1,0:T(8,128)} %update_at.1, f32[512,128]{1,0:T(8,128)} %parent_at.1, bf16[2,256,512]{2,1,0:T(8,128)(2,1)} %lower_pivot_at.1, bf16[512,512]{1,0:T(8,128)(2,1)} %lower_update_at.1, ...), custom_call_target="tpu_custom_call" | custom-call | tf_op jit(solution)/shard_map/pallas_call | solution.py:968
  78.4 0.7 copy.14
  79.1 0.7 copy.15

commit v6 on v5

--- a/solution.py
+++ b/solution.py
@@ -636,7 +636,24 @@
                     guard(both(self.keep(group, goal), elsewhere), functools.partial(action, step, side))
 
         def start(self, q):
-            self.sends(lambda step, side: self.copy(q, step, side).start())
+            self.start_far(q)
+            self.start_near(q)
+
+        def start_far(self, q):
+            def action(step, side):
+                @pl.when(self.plane(step) != group)
+                def _():
+                    self.copy(q, step, side).start()
+
+            self.sends(action)
+
+        def start_near(self, q):
+            def action(step, side):
+                @pl.when(self.plane(step) == group)
+                def _():
+                    self.copy(q, step, side).start()
+
+            self.sends(action)
 
             @pl.when(group == me_r)
             def _():
@@ -885,6 +902,7 @@
                 spread(scatter, q, value, m)
 
             guard(gather.active, action)
+        for q in chunks:
             with jax.named_scope(name + "_add"):
                 scatter.add(q, sum_par.at[level + 1, q])
             vec[level + 1, q] = sum_par[level + 1, q].astype(BF)
@@ -894,10 +912,12 @@
         with jax.named_scope("piv_add"):
             t_piv.add(q, sum_piv.at[0, q])
         phalf[q] = sum_piv[0, q].astype(BF)
-        g_half.start(q)
+        g_half.start_far(q)
 
     parent(0, g_low, t_low, parent_lower, g_up, "low")
 
+    for q in chunks:
+        g_half.start_near(q)
     parent(1, g_up, t_high, parent_upper, g_all, "up")
 
     ready(upper_pivot)

time: 80.5 us -> 79.7 us (0.990)
  no operation moved by 1% of the time
where the time goes in v6:
time: 79.7 us; the launch traced here: 79.2 us
  Pallas kernels  77.1 us (97%)
  local copies, waits for them, and re-layouts  1.41 us (2%)
    pallas_call x1, Pallas kernels, shards(): pl.pallas_call(functools.partial(split_kernel, panels, cols), out_shape=(...  77.1 us

profile of v6, /device:TPU:0, one launch (start us, length us, event | category | flops | bytes accessed | tf_op | source)
XLA Modules:
  0.0 79.2 jit_solution(1725734834377435295)
XLA Ops:
  0.6 77.1 %shard_map.113 = (f32[512,128]{1,0:T(8,128)S(1)}, f32[2,256,128]{2,1,0:T(8,128)S(1)}) custom-call(f32[2,256,128]{2,1,0:T(8,128)} %pivot_at.1, f32[512,128]{1,0:T(8,128)} %update_at.1, f32[512,128]{1,0:T(8,128)} %parent_at.1, bf16[2,256,512]{2,1,0:T(8,128)(2,1)} %lower_pivot_at.1, bf16[512,512]{1,0:T(8,128)(2,1)} %lower_update_at.1, ...), custom_call_target="tpu_custom_call" | custom-call | tf_op jit(solution)/shard_map/pallas_call | solution.py:988
  77.8 0.7 copy.14
  78.5 0.7 copy.15
